TPU v7x, 32 devices: a whole 2x2x4 slice. The times are simulated.
32 devices in a mesh: gx: 4 (over y, core), gy: 8 (over z, x).
Axes of the slice: x: 2, y: 2, z: 4, core: 2. Of those that a mesh axis runs over, the one named last changes fastest.
Arguments:
- previous: float32 [2, 7, 512, 1024], P(None, None, 'gx', 'gy'), may hold values from -6 to 6
- dissipated: float32 [2, 4, 512, 1024], P(None, None, 'gx', 'gy'), may hold values from 0.05 to 3
- material: int32 [4, 512, 1024], P(None, 'gx', 'gy'), may hold values from 0 to 3
- coolant: int32 [3, 512, 1024], P(None, 'gx', 'gy'), may hold values from 0 to 3
Outputs:
- temperature: float32 [2, 7, 512, 1024], P(None, None, 'gx', 'gy')
All inputs are finite; a program needn't handle non-finite values.
Results may differ from a plain program's by a relative error of at most 0.00011.
Values sent between devices are 32-bit elements; how exact they have to be, the bound alone decides.
A program may use at most 64 MiB of HBM per device.

v0:
```python
import functools
import math

import jax
import jax.numpy as jnp
from jax import lax
from jax.experimental import pallas as pl
from jax.experimental.pallas import tpu as pltpu
from jax.sharding import PartitionSpec as P

ITERS = 3
TIER_K = (1.0, 0.3, 0.12, 2.5)
CHANNEL_K = (1.0, 0.3, 0.25, 0.2)
CHANNEL_SINK = (0.0, 0.15, 0.45, 1.2)
TIER_HEAT = 0.05
CHANNEL_HEAT = 0.2
VERTICAL = 4.0

HALO = 8
STRIP = 4
SLOT = 2 * STRIP
MESH = pl.DeviceIdType.MESH

TIER_ROOT = tuple(math.sqrt(v) for v in TIER_K)
CHANNEL_ROOT = tuple(math.sqrt(v) for v in CHANNEL_K)
TIER_INV = tuple(1.0 / math.sqrt(v) for v in TIER_K)
CHANNEL_INV = tuple(1.0 / math.sqrt(v) for v in CHANNEL_K)


def lookup(codes, table):
    total = jnp.zeros(codes.shape, jnp.float32)
    for index, value in enumerate(table):
        total = jnp.where(codes == index, jnp.float32(value), total)
    return total


def coefficients(nu):
    def inner(a, b):
        total = None
        for i, x in enumerate(a):
            for j, y in enumerate(b):
                term = x * y * nu[i + j]
                total = term if total is None else total + term
        return total

    zero = nu[0] * 0.0
    rho = [zero + 1.0]
    pi = [zero + 1.0]
    norm = nu[0]
    result = [zero] * ITERS
    for iteration in range(ITERS):
        image = [a - b for a, b in zip(pi + [zero], [zero] + pi)]
        step = norm / inner(pi, image)
        for i, a in enumerate(pi):
            result[i] = result[i] + step * a
        if iteration + 1 < ITERS:
            rho = [a - step * b for a, b in zip(rho + [zero], image)]
            following = inner(rho, rho)
            growth = following / norm
            pi = [a + growth * b for a, b in zip(rho, pi + [zero])]
            norm = following
    return result


def kernel(nx, ny, prev, diss, mat, cool, out, vp, vq, vm, vc, own_l, own_r, far_l, far_r,
           edges, root, weight, capac, up, u0, u1, u2, result, row, rows,
           picks, split, load_sem, send_sem, recv_sem, row_send, row_recv, store_sem):
    scen, layers, length, width = prev.shape
    tiers = mat.shape[0]
    n = nx * ny
    ext = length + 2 * HALO
    x, y = lax.axis_index("gx"), lax.axis_index("gy")
    me = x * ny + y
    barrier = pltpu.get_barrier_semaphore()

    def other(i):
        k = lax.rem(me + i, n)
        return k // ny, lax.rem(k, ny)

    def greet(i, carry):
        pl.semaphore_signal(barrier, inc=1, device_id=other(i), device_id_type=MESH)
        return carry

    inside = pl.ds(HALO, length)
    loads = [
        pltpu.make_async_copy(prev, vp.at[:, :, inside], load_sem.at[0]),
        pltpu.make_async_copy(diss, vq.at[:, :, inside], load_sem.at[1]),
        pltpu.make_async_copy(mat, vm.at[:, inside], load_sem.at[2]),
        pltpu.make_async_copy(cool, vc.at[:, inside], load_sem.at[3]),
    ]
    for copy in loads:
        copy.start()
    lax.fori_loop(1, n, greet, 0)

    has = {(-1, 0): x > 0, (1, 0): x < nx - 1, (0, -1): y > 0, (0, 1): y < ny - 1}
    for dx in (-1, 1):
        for dy in (-1, 1):
            has[dx, dy] = jnp.logical_and(has[dx, 0], has[0, dy])
    top, bottom = pl.ds(0, HALO), pl.ds(HALO + length, HALO)
    first, last = pl.ds(HALO, HALO), pl.ds(length, HALO)

    def fill(ref):
        ref[...] = jnp.full(ref.shape, -1, ref.dtype)

    for dx, where in ((-1, top), (1, bottom)):
        @pl.when(jnp.logical_not(has[dx, 0]))
        def _(where=where):
            for ref in (vp, vq):
                fill(ref.at[:, :, where])
            for ref in (vm, vc):
                fill(ref.at[:, where])
            fill(own_l.at[where])
            fill(own_r.at[where])
    for dy, ref in ((-1, far_l), (1, far_r)):
        @pl.when(jnp.logical_not(has[0, dy]))
        def _(ref=ref):
            fill(ref.at[inside])
        for dx, where in ((-1, top), (1, bottom)):
            @pl.when(jnp.logical_not(has[dx, dy]))
            def _(ref=ref, where=where):
                fill(ref.at[where])

    for copy in loads:
        copy.wait()

    places = []
    for s in range(scen):
        for layer in range(layers):
            places.append((SLOT * (s * layers + layer), vp, (s, layer)))
    for layer in range(layers):
        ref = vm if layer % 2 == 0 else vc
        places.append((SLOT * layer + STRIP, ref, (layer // 2,)))
    for t in range(tiers):
        places.append((SLOT * (layers + 1 + 2 * t) + STRIP, vq, (0, t)))
        places.append((SLOT * (layers + 2 * t) + STRIP, vq, (1, t)))
    chunk = 4 * HALO

    def pack(step, carry):
        start = pl.multiple_of(HALO + step * chunk, HALO)
        lane = lax.broadcasted_iota(jnp.int32, (chunk, width), 1)
        left = jnp.zeros((chunk, width), jnp.float32)
        right = jnp.zeros((chunk, width), jnp.float32)
        for base, ref, index in places:
            plane = ref[index + (pl.ds(start, chunk),)].astype(jnp.float32)
            turned = pltpu.roll(plane, base, 1) if base else plane
            left = jnp.where((lane >= base) & (lane < base + STRIP), turned, left)
            low = (base - STRIP) % width
            right = jnp.where((lane >= low) & (lane < low + STRIP), turned, right)
        own_l[pl.ds(start, chunk)] = left
        own_r[pl.ds(start, chunk)] = pltpu.roll(right, STRIP, 1)
        return carry

    lax.fori_loop(0, length // chunk, pack, 0)

    def pick(slot, carry):
        near = (2 * width, width)
        source = lax.broadcasted_iota(jnp.int32, near, 0) % width - SLOT * slot
        target = lax.broadcasted_iota(jnp.int32, near, 1)
        west = (source == STRIP - 1) & (target == 0)
        east = (source == STRIP - 2) & (target == width - 1)
        picks[slot] = jnp.where(west | east, 1.0, 0.0).astype(jnp.bfloat16)
        return carry

    lax.fori_loop(0, scen * layers, pick, 0)

    pl.semaphore_wait(barrier, n - 1)

    sends = []
    for dx, source, target in ((-1, first, bottom), (1, last, top)):
        for ref in (vp, vq):
            sends.append((dx, 0, ref.at[:, :, source], ref.at[:, :, target]))
        for ref in (vm, vc):
            sends.append((dx, 0, ref.at[:, source], ref.at[:, target]))
        for ref in (own_l, own_r):
            sends.append((dx, 0, ref.at[source], ref.at[target]))
        sends.append((dx, -1, own_l.at[source], far_r.at[target]))
        sends.append((dx, 1, own_r.at[source], far_l.at[target]))
    sends.append((0, -1, own_l.at[inside], far_r.at[inside]))
    sends.append((0, 1, own_r.at[inside], far_l.at[inside]))
    copies = []
    for i, (dx, dy, source, target) in enumerate(sends):
        copy = pltpu.make_async_remote_copy(
            src_ref=source, dst_ref=target, send_sem=send_sem.at[i], recv_sem=recv_sem.at[i],
            device_id=(x + dx, y + dy), device_id_type=MESH)
        copies.append((dx, dy, copy))
    order = sorted(copies, key=lambda c: 0 if c[0] == 0 else 1 if c[1] == 0 else 2)
    for dx, dy, copy in order:
        @pl.when(has[dx, dy])
        def _(copy=copy):
            copy.start()
    blank = jnp.zeros((ext + 2 * HALO, width), jnp.float32)
    for pad in (0, layers + 1):
        root[pad] = blank
        for s in range(scen):
            for ref in (up, u0, u1, u2):
                ref[s, pad] = blank

    def prepare(begin, count):
        at, to = pl.ds(begin, count), pl.ds(begin + HALO, count)
        for layer in range(layers):
            if layer % 2 == 0:
                s = lookup(vm[layer // 2, at], TIER_ROOT)
                total = jnp.full((count, width), TIER_HEAT, jnp.float32)
            else:
                codes = vc[layer // 2, at]
                s = lookup(codes, CHANNEL_ROOT)
                total = CHANNEL_HEAT + lookup(codes, CHANNEL_SINK)
            root[layer + 1, to] = s
            capac[layer, at] = total
            for k in range(scen):
                up[k, layer + 1, to] = s * vp[k, layer, at]

    prepare(HALO, length)
    body = pl.ds(HALO, ext)

    def stencil(ref, at, layer, edge, slot, start=0, count=ext):
        lane = lax.broadcasted_iota(jnp.int32, (count, width), 1)
        rows_at = pl.ds(HALO + start, count)
        centre = ref[at + (layer + 1, rows_at)]
        west = jnp.where(lane == 0, 0.0, pltpu.roll(centre, 1, 1))
        east = jnp.where(lane == width - 1, 0.0, pltpu.roll(centre, width - 1, 1))
        lateral = west + east + ref[at + (layer + 1, pl.ds(HALO + start - 1, count))]
        lateral = lateral + ref[at + (layer + 1, pl.ds(HALO + start + 1, count))]
        vertical = ref[at + (layer, rows_at)] + ref[at + (layer + 2, rows_at)]
        around = lateral + VERTICAL * vertical
        if edge is not None:
            around = around + border(edge, slot, start, count)
        return centre, around

    def border(edge, slot, start, count):
        return jnp.dot(split[edge, pl.ds(start, count)], picks[slot],
                       preferred_element_type=jnp.float32)

    inner, rest = 2 * HALO, length - 2 * HALO

    def early(layer, carry):
        at = pl.ds(inner, rest)
        weight[layer, at] = stencil(root, (), layer, None, 0, inner, rest)[1]
        for k in range(scen):
            u1[k, layer + 1, at] = stencil(up, (k,), layer, None, 0, inner, rest)[1]
        return carry

    lax.fori_loop(0, layers, early, 0)

    for dx, dy, copy in copies:
        @pl.when(has[-dx, -dy])
        def _(copy=copy):
            copy.wait_recv()

    prepare(0, HALO)
    prepare(HALO + length, HALO)

    shape = (ext, width)
    lane = lax.broadcasted_iota(jnp.int32, shape, 1)
    place = lane // SLOT
    low = lane % SLOT < STRIP
    layer_of = place % layers
    tier = layer_of % 2 == 0
    used = place < scen * layers

    def strip_stencil(u):
        lateral = pltpu.roll(u, 1, 1) + pltpu.roll(u, width - 1, 1)
        lateral = lateral + pltpu.roll(u, 1, 0) + pltpu.roll(u, ext - 1, 0)
        above = jnp.where(layer_of > 0, pltpu.roll(u, SLOT, 1), 0.0)
        below = jnp.where(layer_of < layers - 1, pltpu.roll(u, width - SLOT, 1), 0.0)
        return lateral + VERTICAL * (above + below)

    def strip(field, rest):
        codes = jnp.where(place < layers, rest, pltpu.roll(rest, SLOT * layers, 1))
        codes = jnp.where(used, codes, -1.0)
        power = jnp.where(place < layers, pltpu.roll(rest, width - SLOT * (layers + 1), 1), rest)
        power = jnp.where(tier & used, power, 0.0)
        s = jnp.where(tier, lookup(codes, TIER_ROOT), lookup(codes, CHANNEL_ROOT))
        heat = jnp.where(tier, TIER_HEAT, CHANNEL_HEAT)
        total = heat + jnp.where(tier, 0.0, lookup(codes, CHANNEL_SINK))
        total = total + s * strip_stencil(s)
        inverse = 1.0 / total
        scaled = s * field
        residual = (heat - total) * field + power + s * strip_stencil(scaled)
        w = s * s * inverse
        a = s * residual * inverse
        b = w * strip_stencil(a)
        c = w * strip_stencil(b)
        return s, scaled, a, b, c

    here, there = own_l[...], far_l[...]
    lefts = strip(jnp.where(low, there, pltpu.roll(here, STRIP, 1)),
                  jnp.where(low, pltpu.roll(there, width - STRIP, 1), here))
    for i, value in enumerate(lefts):
        edges[i] = value
    here, there = own_r[...], far_r[...]
    rights = strip(jnp.where(low, here, pltpu.roll(there, STRIP, 1)),
                   jnp.where(low, pltpu.roll(here, width - STRIP, 1), there))
    for i, value in enumerate(rights):
        both = jnp.where(lane % SLOT == STRIP - 1, edges[i], pltpu.roll(value, width - 2, 1))
        high = both.astype(jnp.bfloat16)
        split[i, :, :width] = high
        split[i, :, width:] = (both - high.astype(jnp.float32)).astype(jnp.bfloat16)

    body = pl.ds(HALO, ext)

    def gather(total, value):
        tiles = value[HALO:HALO + length].reshape(length // HALO, HALO, width)
        return total + jnp.sum(tiles, axis=0)

    none = jnp.zeros((HALO, width), jnp.float32)

    def begin(layer, carry):
        is_tier = lax.rem(layer, 2) == 0
        heat = jnp.where(is_tier, jnp.float32(TIER_HEAT), jnp.float32(CHANNEL_HEAT))
        on = jnp.where(is_tier, jnp.float32(1.0), jnp.float32(0.0))
        sums = list(carry)
        for start, count in ((0, inner), (inner, rest), (inner + rest, inner)):
            at = pl.ds(start, count)
            if start == inner:
                s = root[layer + 1, pl.ds(HALO + start, count)]
                around = weight[layer, at] + border(0, layer, start, count)
            else:
                s, around = stencil(root, (), layer, 0, layer, start, count)
            total = capac[layer, at] + s * around
            inverse = 1.0 / total
            weight[layer, at] = s * s * inverse
            for k in range(scen):
                slot = k * layers + layer
                if start == inner:
                    around = u1[k, layer + 1, at] + border(1, slot, start, count)
                else:
                    _, around = stencil(up, (k,), layer, 1, slot, start, count)
                residual = (heat - total) * vp[k, layer, at] + on * vq[k, layer // 2, at]
                residual = residual + s * around
                scaled = residual * inverse
                u0[k, layer + 1, pl.ds(HALO + start, count)] = s * scaled
                own = residual * scaled
                own = own[HALO:] if start == 0 else own[:HALO] if start > inner else own
                sums[k] = sums[k] + jnp.sum(own.reshape(-1, HALO, width), axis=0)
        return tuple(sums)

    def advance(source, target, edge):
        def one(layer, carry):
            sums = []
            for k in range(scen):
                centre, around = stencil(source, (k,), layer, edge, k * layers + layer)
                sums.append(gather(carry[len(sums)], centre * around))
                if target is not None:
                    moved = weight[layer] * around
                    target[k, layer + 1, body] = moved
                    sums.append(gather(carry[len(sums)], moved * around))
            return tuple(sums)

        count = scen * (1 if target is None else 2)
        return lax.fori_loop(0, layers, one, (none,) * count, unroll=True)

    first_sums = lax.fori_loop(0, layers, begin, (none,) * scen, unroll=True)
    second = advance(u0, u1, 2)
    third = advance(u1, u2, 3)
    fourth = advance(u2, None, 4)
    moments = []
    for k in range(scen):
        moments += [first_sums[k], *second[2 * k:2 * k + 2], *third[2 * k:2 * k + 2], fourth[k]]
    count = len(moments)
    flat = jnp.zeros((1, width), jnp.float32)
    line = lax.broadcasted_iota(jnp.int32, (1, width), 1)
    for i, value in enumerate(moments):
        total = jnp.sum(jnp.sum(value, axis=0, keepdims=True), axis=1, keepdims=True)
        flat = jnp.where(line == i, total, flat)
    row[...] = flat
    rows[n - 1] = flat

    def to(i):
        return pltpu.make_async_remote_copy(
            src_ref=row, dst_ref=rows.at[i - 1], send_sem=row_send, recv_sem=row_recv,
            device_id=other(i), device_id_type=MESH)

    def spread(i, carry):
        to(i).start()
        return carry

    lax.fori_loop(1, n, spread, 0)
    for dx, dy, copy in copies:
        @pl.when(has[dx, dy])
        def _(copy=copy):
            copy.wait_send()
    own = pl.ds(2 * HALO, length)
    for layer in range(layers):
        if layer % 2 == 0:
            back = lookup(vm[layer // 2, inside], TIER_INV)
        else:
            back = lookup(vc[layer // 2, inside], CHANNEL_INV)
        for k in range(scen):
            for ref in (u0, u1, u2):
                ref[k, layer + 1, own] = back * ref[k, layer + 1, own]
    arrived = rows.at[pl.ds(0, n - 1)]
    pltpu.make_async_copy(arrived, arrived, row_recv).wait()
    summed = jnp.sum(rows[...], axis=0)
    total = [jnp.sum(jnp.where(line == i, summed, 0.0), axis=1, keepdims=True)
             for i in range(count)]
    each = count // scen
    for k in range(scen):
        c0, c1, c2 = coefficients(total[k * each:(k + 1) * each])
        for layer in range(layers):
            change = c0 * u0[k, layer + 1, own] + c1 * u1[k, layer + 1, own]
            change = change + c2 * u2[k, layer + 1, own]
            result[k, layer] = vp[k, layer, inside] + change
            pltpu.make_async_copy(result.at[k, layer], out.at[k, layer], store_sem).start()
    pltpu.make_async_copy(result, out, store_sem).wait()
    pltpu.make_async_copy(arrived, arrived, row_send).wait()


def per_device(nx, ny, previous, dissipated, material, coolant):
    scen, layers, length, width = previous.shape
    tiers = material.shape[0]
    ext = length + 2 * HALO
    f32 = jnp.float32
    field = pltpu.VMEM((scen, layers + 2, ext + 2 * HALO, width), f32)
    strip = pltpu.VMEM((ext, width), f32)
    return pl.pallas_call(
        functools.partial(kernel, nx, ny),
        out_shape=jax.ShapeDtypeStruct(previous.shape, f32),
        in_specs=[pl.BlockSpec(memory_space=pl.ANY)] * 4,
        out_specs=pl.BlockSpec(memory_space=pl.ANY),
        scratch_shapes=[
            pltpu.VMEM((scen, layers, ext, width), f32),
            pltpu.VMEM((scen, tiers, ext, width), f32),
            pltpu.VMEM((tiers, ext, width), jnp.int32),
            pltpu.VMEM((layers - tiers, ext, width), jnp.int32),
            strip, strip, strip, strip,
            pltpu.VMEM((5, ext, width), f32),
            pltpu.VMEM((layers + 2, ext + 2 * HALO, width), f32),
            pltpu.VMEM((layers, ext, width), f32),
            pltpu.VMEM((layers, ext, width), f32),
            field, field, field, field,
            pltpu.VMEM(previous.shape, f32),
            pltpu.VMEM((1, width), f32),
            pltpu.VMEM((nx * ny, 1, width), f32),
            pltpu.VMEM((scen * layers, 2 * width, width), jnp.bfloat16),
            pltpu.VMEM((5, ext, 2 * width), jnp.bfloat16),
            pltpu.SemaphoreType.DMA((4,)),
            pltpu.SemaphoreType.DMA((18,)),
            pltpu.SemaphoreType.DMA((18,)),
            pltpu.SemaphoreType.DMA,
            pltpu.SemaphoreType.DMA,
            pltpu.SemaphoreType.DMA,
        ],
        compiler_params=pltpu.CompilerParams(
            collective_id=0, has_side_effects=True, vmem_limit_bytes=56 * 1024 * 1024),
    )(previous, dissipated, material, coolant)


def solution(mesh):
    return jax.shard_map(
        functools.partial(per_device, mesh.shape["gx"], mesh.shape["gy"]),
        mesh=mesh,
        in_specs=(
            P(None, None, "gx", "gy"),
            P(None, None, "gx", "gy"),
            P(None, "gx", "gy"),
            P(None, "gx", "gy"),
        ),
        out_specs=P(None, None, "gx", "gy"),
        check_vma=False,
    )
```

profile of v0, /device:TPU:0, one launch (start us, length us, event | category | flops | bytes accessed | tf_op | source)
XLA Modules:
  0.0 24.0 jit_solution(13782849039287342867)
XLA Ops:
  0.0 21.8 %shard_map.46 = f32[2,7,128,128]{3,2,1,0:T(8,128)} custom-call(f32[2,7,128,128]{3,2,1,0:T(8,128)} %prev.1, f32[2,4,128,128]{3,2,1,0:T(8,128)} %diss.1, s32[4,128,128]{2,1,0:T(8,128)} %mat.1, s32[3,128,128]{2,1,0:T(8,128)} %cool.1), custom_call_target="tpu_custom_call" | custom-call | tf_op jit(solution)/shard_map/pallas_call | solution.py:416
  21.8 2.2 %copy.6 = f32[2,7,128,128]{3,2,1,0:T(8,128)} copy(f32[2,7,128,128]{3,2,1,0:T(8,128)} %shard_map.46) | data formatting | bytes 1835008
where the time goes:
time: 24.2 us; the launch traced here: 24 us
  Pallas kernels  21.8 us (90%)
  local copies, waits for them, and re-layouts  2.18 us (9%)
    pallas_call x1, Pallas kernels, per_device(): pl.pallas_call(functools.partial(kernel, nx, ny), out_shape=jax.ShapeDtyp...  21.8 us
    unnamed x1, local copies, waits for them, and re-layouts  2.18 us

commit v1 on v0

--- a/solution.py
+++ b/solution.py
@@ -63,8 +63,8 @@
 
 
 def kernel(nx, ny, prev, diss, mat, cool, out, vp, vq, vm, vc, own_l, own_r, far_l, far_r,
-           edges, root, weight, capac, up, u0, u1, u2, result, row, rows,
-           picks, split, load_sem, send_sem, recv_sem, row_send, row_recv, store_sem):
+           edges, root, weight, capac, up, u0, u1, u2, row, rows,
+           picks, split, load_sem, send_sem, recv_sem, row_send, row_recv):
     scen, layers, length, width = prev.shape
     tiers = mat.shape[0]
     n = nx * ny
@@ -400,9 +400,7 @@
         for layer in range(layers):
             change = c0 * u0[k, layer + 1, own] + c1 * u1[k, layer + 1, own]
             change = change + c2 * u2[k, layer + 1, own]
-            result[k, layer] = vp[k, layer, inside] + change
-            pltpu.make_async_copy(result.at[k, layer], out.at[k, layer], store_sem).start()
-    pltpu.make_async_copy(result, out, store_sem).wait()
+            out[k, layer] = vp[k, layer, inside] + change
     pltpu.make_async_copy(arrived, arrived, row_send).wait()
 
 
@@ -415,9 +413,9 @@
     strip = pltpu.VMEM((ext, width), f32)
     return pl.pallas_call(
         functools.partial(kernel, nx, ny),
-        out_shape=jax.ShapeDtypeStruct(previous.shape, f32),
+        out_shape=pltpu.VMEM(previous.shape, f32),
         in_specs=[pl.BlockSpec(memory_space=pl.ANY)] * 4,
-        out_specs=pl.BlockSpec(memory_space=pl.ANY),
+        out_specs=pl.BlockSpec(memory_space=pltpu.VMEM),
         scratch_shapes=[
             pltpu.VMEM((scen, layers, ext, width), f32),
             pltpu.VMEM((scen, tiers, ext, width), f32),
@@ -429,7 +427,6 @@
             pltpu.VMEM((layers, ext, width), f32),
             pltpu.VMEM((layers, ext, width), f32),
             field, field, field, field,
-            pltpu.VMEM(previous.shape, f32),
             pltpu.VMEM((1, width), f32),
             pltpu.VMEM((nx * ny, 1, width), f32),
             pltpu.VMEM((scen * layers, 2 * width, width), jnp.bfloat16),
@@ -439,10 +436,9 @@
             pltpu.SemaphoreType.DMA((18,)),
             pltpu.SemaphoreType.DMA,
             pltpu.SemaphoreType.DMA,
-            pltpu.SemaphoreType.DMA,
         ],
         compiler_params=pltpu.CompilerParams(
-            collective_id=0, has_side_effects=True, vmem_limit_bytes=56 * 1024 * 1024),
+            collective_id=0, has_side_effects=True, vmem_limit_bytes=60 * 1024 * 1024),
     )(previous, dissipated, material, coolant)
 
 

time: 24.2 us -> 22.2 us (0.917)
  local copies, waits for them, and re-layouts: 2.18 us -> 0.93 us
  Pallas kernels: 21.8 us -> 21.1 us
    unnamed x1, local copies, waits for them, and re-layouts: 2.18 us -> 0.93 us
    pallas_call x1, Pallas kernels: 21.8 us -> 21.1 us  [per_device(): pl.pallas_call(functools.partial(kernel, nx, ny), out_shape=pltpu.VMEM(pr...]
where the time goes in v1:
time: 22.2 us; the launch traced here: 22 us
  Pallas kernels  21.1 us (95%)
  local copies, waits for them, and re-layouts  0.93 us (4%)
    pallas_call x1, Pallas kernels, per_device(): pl.pallas_call(functools.partial(kernel, nx, ny), out_shape=pltpu.VMEM(pr...  21.1 us
    unnamed x1, local copies, waits for them, and re-layouts  0.93 us

profile of v1, /device:TPU:0, one launch (start us, length us, event | category | flops | bytes accessed | tf_op | source)
XLA Modules:
  0.0 22.0 jit_solution(222551551069286742)
XLA Ops:
  0.0 21.1 %shard_map.46 = f32[2,7,128,128]{3,2,1,0:T(8,128)S(1)} custom-call(f32[2,7,128,128]{3,2,1,0:T(8,128)} %prev.1, f32[2,4,128,128]{3,2,1,0:T(8,128)} %diss.1, s32[4,128,128]{2,1,0:T(8,128)} %mat.1, s32[3,128,128]{2,1,0:T(8,128)} %cool.1), custom_call_target="tpu_custom_call" | custom-call | tf_op jit(solution)/shard_map/pallas_call | solution.py:414
  21.1 0.9 %copy.6 = f32[2,7,128,128]{3,2,1,0:T(8,128)} copy(f32[2,7,128,128]{3,2,1,0:T(8,128)S(1)} %shard_map.46) | data formatting | bytes 1835008

commit v2 on v1

--- a/solution.py
+++ b/solution.py
@@ -64,7 +64,7 @@
 
 def kernel(nx, ny, prev, diss, mat, cool, out, vp, vq, vm, vc, own_l, own_r, far_l, far_r,
            edges, root, weight, capac, up, u0, u1, u2, row, rows,
-           picks, split, load_sem, send_sem, recv_sem, row_send, row_recv):
+           along, across, known, load_sem, send_sem, recv_sem, row_send, row_recv):
     scen, layers, length, width = prev.shape
     tiers = mat.shape[0]
     n = nx * ny
@@ -73,13 +73,36 @@
     me = x * ny + y
     barrier = pltpu.get_barrier_semaphore()
 
-    def other(i):
-        k = lax.rem(me + i, n)
-        return k // ny, lax.rem(k, ny)
-
-    def greet(i, carry):
-        pl.semaphore_signal(barrier, inc=1, device_id=other(i), device_id_type=MESH)
-        return carry
+    def around_me(reach):
+        found = []
+        for dx in (-reach, 0, reach):
+            for dy in (-reach, 0, reach):
+                if (dx or dy) and abs(dx) < nx and abs(dy) < ny:
+                    inside_x = jnp.logical_and(x + dx >= 0, x + dx < nx)
+                    inside_y = jnp.logical_and(y + dy >= 0, y + dy < ny)
+                    found.append((dx, dy, jnp.logical_and(inside_x, inside_y)))
+        return found
+
+    def greet(sem, reach):
+        for dx, dy, there in around_me(reach):
+            @pl.when(there)
+            def _(dx=dx, dy=dy):
+                pl.semaphore_signal(sem, inc=1, device_id=(x + dx, y + dy), device_id_type=MESH)
+
+    def hear(sem, reach):
+        pl.semaphore_wait(sem, sum(there.astype(jnp.int32) for _, _, there in around_me(reach)))
+
+    reaches = [1]
+    while 2 * reaches[-1] < max(nx, ny) - 1:
+        reaches.append(2 * reaches[-1])
+    heard = []
+
+    def know():
+        if len(heard) < len(reaches):
+            hear(known.at[len(heard)], reaches[len(heard)])
+            heard.append(True)
+            if len(heard) < len(reaches):
+                greet(known.at[len(heard)], reaches[len(heard)])
 
     inside = pl.ds(HALO, length)
     loads = [
@@ -88,9 +111,9 @@
         pltpu.make_async_copy(mat, vm.at[:, inside], load_sem.at[2]),
         pltpu.make_async_copy(cool, vc.at[:, inside], load_sem.at[3]),
     ]
-    for copy in loads:
+    for copy in reversed(loads):
         copy.start()
-    lax.fori_loop(1, n, greet, 0)
+    greet(barrier, 1)
 
     has = {(-1, 0): x > 0, (1, 0): x < nx - 1, (0, -1): y > 0, (0, 1): y < ny - 1}
     for dx in (-1, 1):
@@ -120,50 +143,42 @@
             def _(ref=ref, where=where):
                 fill(ref.at[where])
 
-    for copy in loads:
-        copy.wait()
-
-    places = []
+    first_places, later_places = [], []
+    for layer in range(layers):
+        ref = vm if layer % 2 == 0 else vc
+        first_places.append((SLOT * layer, ref, (layer // 2,)))
+    for t in range(tiers):
+        first_places.append((SLOT * (layers + 1 + 2 * t), vq, (0, t)))
+        first_places.append((SLOT * (layers + 2 * t), vq, (1, t)))
     for s in range(scen):
         for layer in range(layers):
-            places.append((SLOT * (s * layers + layer), vp, (s, layer)))
-    for layer in range(layers):
-        ref = vm if layer % 2 == 0 else vc
-        places.append((SLOT * layer + STRIP, ref, (layer // 2,)))
-    for t in range(tiers):
-        places.append((SLOT * (layers + 1 + 2 * t) + STRIP, vq, (0, t)))
-        places.append((SLOT * (layers + 2 * t) + STRIP, vq, (1, t)))
-    chunk = 4 * HALO
-
-    def pack(step, carry):
-        start = pl.multiple_of(HALO + step * chunk, HALO)
-        lane = lax.broadcasted_iota(jnp.int32, (chunk, width), 1)
-        left = jnp.zeros((chunk, width), jnp.float32)
-        right = jnp.zeros((chunk, width), jnp.float32)
-        for base, ref, index in places:
-            plane = ref[index + (pl.ds(start, chunk),)].astype(jnp.float32)
-            turned = pltpu.roll(plane, base, 1) if base else plane
-            left = jnp.where((lane >= base) & (lane < base + STRIP), turned, left)
-            low = (base - STRIP) % width
-            right = jnp.where((lane >= low) & (lane < low + STRIP), turned, right)
-        own_l[pl.ds(start, chunk)] = left
-        own_r[pl.ds(start, chunk)] = pltpu.roll(right, STRIP, 1)
-        return carry
-
-    lax.fori_loop(0, length // chunk, pack, 0)
-
-    def pick(slot, carry):
-        near = (2 * width, width)
-        source = lax.broadcasted_iota(jnp.int32, near, 0) % width - SLOT * slot
-        target = lax.broadcasted_iota(jnp.int32, near, 1)
-        west = (source == STRIP - 1) & (target == 0)
-        east = (source == STRIP - 2) & (target == width - 1)
-        picks[slot] = jnp.where(west | east, 1.0, 0.0).astype(jnp.bfloat16)
-        return carry
-
-    lax.fori_loop(0, scen * layers, pick, 0)
-
-    pl.semaphore_wait(barrier, n - 1)
+            later_places.append((SLOT * (s * layers + layer), vp, (s, layer)))
+
+    def pack(places):
+        lane = lax.broadcasted_iota(jnp.int32, (length, width), 1)
+        left = right = opening = None
+        for base, ref, index in sorted(places, key=lambda place: place[0]):
+            plane = ref[index + (inside,)].astype(jnp.float32)
+            if base == 0:
+                left = right = opening = plane
+            else:
+                turned = pltpu.roll(plane, base, 1)
+                left = jnp.where(lane >= base, turned, left)
+                right = jnp.where(lane >= base - STRIP, turned, right)
+        return left, jnp.where(lane >= width - STRIP, opening, right)
+
+    for copy in loads[1:]:
+        copy.wait()
+    own_l[inside], own_r[inside] = pack(first_places)
+    loads[0].wait()
+    left, right = pack(later_places)
+    low = lax.broadcasted_iota(jnp.int32, (length, width), 1) % SLOT < STRIP
+    own_l[inside] = jnp.where(low, left, pltpu.roll(own_l[inside], STRIP, 1))
+    low = (lax.broadcasted_iota(jnp.int32, (length, width), 1) + STRIP) % SLOT < STRIP
+    own_r[inside] = pltpu.roll(jnp.where(low, right, pltpu.roll(own_r[inside], STRIP, 1)), STRIP, 1)
+
+    hear(barrier, 1)
+    greet(known.at[0], 1)
 
     sends = []
     for dx, source, target in ((-1, first, bottom), (1, last, top)):
@@ -188,6 +203,19 @@
         @pl.when(has[dx, dy])
         def _(copy=copy):
             copy.start()
+    for i in range(2):
+        source = lax.broadcasted_iota(jnp.int32, (width, width), 0)
+        target = lax.broadcasted_iota(jnp.int32, (width, width), 1)
+        apart = target - source
+        beside = (apart == 1) | (apart == -1)
+        along[pl.ds(i * width, width)] = jnp.where(beside, 1.0, 0.0).astype(jnp.bfloat16)
+        spot = target // SLOT
+        level = spot % layers
+        used = spot < scen * layers
+        beside = beside & (source // SLOT == spot) & used
+        stacked = (apart == SLOT) & (level > 0) | (apart == -SLOT) & (level < layers - 1)
+        weights = jnp.where(stacked & used, VERTICAL, jnp.where(beside, 1.0, 0.0))
+        across[pl.ds(i * width, width)] = weights.astype(jnp.bfloat16)
     blank = jnp.zeros((ext + 2 * HALO, width), jnp.float32)
     for pad in (0, layers + 1):
         root[pad] = blank
@@ -211,25 +239,34 @@
                 up[k, layer + 1, to] = s * vp[k, layer, at]
 
     prepare(HALO, length)
+    know()
     body = pl.ds(HALO, ext)
 
+    def shifted(value, matrix):
+        high = value.astype(jnp.bfloat16)
+        low = (value - high.astype(jnp.float32)).astype(jnp.bfloat16)
+        return jnp.dot(jnp.concatenate([high, low], axis=1), matrix[...],
+                       preferred_element_type=jnp.float32)
+
     def stencil(ref, at, layer, edge, slot, start=0, count=ext):
-        lane = lax.broadcasted_iota(jnp.int32, (count, width), 1)
         rows_at = pl.ds(HALO + start, count)
         centre = ref[at + (layer + 1, rows_at)]
-        west = jnp.where(lane == 0, 0.0, pltpu.roll(centre, 1, 1))
-        east = jnp.where(lane == width - 1, 0.0, pltpu.roll(centre, width - 1, 1))
-        lateral = west + east + ref[at + (layer + 1, pl.ds(HALO + start - 1, count))]
+        lateral = shifted(centre, along) + ref[at + (layer + 1, pl.ds(HALO + start - 1, count))]
         lateral = lateral + ref[at + (layer + 1, pl.ds(HALO + start + 1, count))]
         vertical = ref[at + (layer, rows_at)] + ref[at + (layer + 2, rows_at)]
         around = lateral + VERTICAL * vertical
         if edge is not None:
-            around = around + border(edge, slot, start, count)
+            around = around + margins(edge, slot, start, count)
         return centre, around
 
     def border(edge, slot, start, count):
-        return jnp.dot(split[edge, pl.ds(start, count)], picks[slot],
-                       preferred_element_type=jnp.float32)
+        shift = (width - SLOT * slot - (STRIP - 1)) % width
+        return pltpu.roll(edges[edge, pl.ds(start, count)], shift, 1)
+
+    def margins(edge, slot, start, count):
+        lane = lax.broadcasted_iota(jnp.int32, (count, width), 1)
+        ends = (lane == 0) | (lane == width - 1)
+        return jnp.where(ends, border(edge, slot, start, count), 0.0)
 
     inner, rest = 2 * HALO, length - 2 * HALO
 
@@ -241,6 +278,7 @@
         return carry
 
     lax.fori_loop(0, layers, early, 0)
+    know()
 
     for dx, dy, copy in copies:
         @pl.when(has[-dx, -dy])
@@ -259,11 +297,7 @@
     used = place < scen * layers
 
     def strip_stencil(u):
-        lateral = pltpu.roll(u, 1, 1) + pltpu.roll(u, width - 1, 1)
-        lateral = lateral + pltpu.roll(u, 1, 0) + pltpu.roll(u, ext - 1, 0)
-        above = jnp.where(layer_of > 0, pltpu.roll(u, SLOT, 1), 0.0)
-        below = jnp.where(layer_of < layers - 1, pltpu.roll(u, width - SLOT, 1), 0.0)
-        return lateral + VERTICAL * (above + below)
+        return shifted(u, across) + pltpu.roll(u, 1, 0) + pltpu.roll(u, ext - 1, 0)
 
     def strip(field, rest):
         codes = jnp.where(place < layers, rest, pltpu.roll(rest, SLOT * layers, 1))
@@ -292,10 +326,7 @@
     rights = strip(jnp.where(low, here, pltpu.roll(there, STRIP, 1)),
                    jnp.where(low, pltpu.roll(here, width - STRIP, 1), there))
     for i, value in enumerate(rights):
-        both = jnp.where(lane % SLOT == STRIP - 1, edges[i], pltpu.roll(value, width - 2, 1))
-        high = both.astype(jnp.bfloat16)
-        split[i, :, :width] = high
-        split[i, :, width:] = (both - high.astype(jnp.float32)).astype(jnp.bfloat16)
+        edges[i] = jnp.where(lane % SLOT == STRIP - 1, edges[i], pltpu.roll(value, width - 2, 1))
 
     body = pl.ds(HALO, ext)
 
@@ -306,15 +337,13 @@
     none = jnp.zeros((HALO, width), jnp.float32)
 
     def begin(layer, carry):
-        is_tier = lax.rem(layer, 2) == 0
-        heat = jnp.where(is_tier, jnp.float32(TIER_HEAT), jnp.float32(CHANNEL_HEAT))
-        on = jnp.where(is_tier, jnp.float32(1.0), jnp.float32(0.0))
+        heat = TIER_HEAT if layer % 2 == 0 else CHANNEL_HEAT
         sums = list(carry)
         for start, count in ((0, inner), (inner, rest), (inner + rest, inner)):
             at = pl.ds(start, count)
             if start == inner:
                 s = root[layer + 1, pl.ds(HALO + start, count)]
-                around = weight[layer, at] + border(0, layer, start, count)
+                around = weight[layer, at] + margins(0, layer, start, count)
             else:
                 s, around = stencil(root, (), layer, 0, layer, start, count)
             total = capac[layer, at] + s * around
@@ -323,10 +352,12 @@
             for k in range(scen):
                 slot = k * layers + layer
                 if start == inner:
-                    around = u1[k, layer + 1, at] + border(1, slot, start, count)
+                    around = u1[k, layer + 1, at] + margins(1, slot, start, count)
                 else:
                     _, around = stencil(up, (k,), layer, 1, slot, start, count)
-                residual = (heat - total) * vp[k, layer, at] + on * vq[k, layer // 2, at]
+                residual = (heat - total) * vp[k, layer, at]
+                if layer % 2 == 0:
+                    residual = residual + vq[k, layer // 2, at]
                 residual = residual + s * around
                 scaled = residual * inverse
                 u0[k, layer + 1, pl.ds(HALO + start, count)] = s * scaled
@@ -347,10 +378,14 @@
                     sums.append(gather(carry[len(sums)], moved * around))
             return tuple(sums)
 
-        count = scen * (1 if target is None else 2)
-        return lax.fori_loop(0, layers, one, (none,) * count, unroll=True)
-
-    first_sums = lax.fori_loop(0, layers, begin, (none,) * scen, unroll=True)
+        carry = (none,) * (scen * (1 if target is None else 2))
+        for layer in range(layers):
+            carry = one(layer, carry)
+        return carry
+
+    first_sums = (none,) * scen
+    for layer in range(layers):
+        first_sums = begin(layer, first_sums)
     second = advance(u0, u1, 2)
     third = advance(u1, u2, 3)
     fourth = advance(u2, None, 4)
@@ -365,14 +400,15 @@
         flat = jnp.where(line == i, total, flat)
     row[...] = flat
     rows[n - 1] = flat
-
-    def to(i):
-        return pltpu.make_async_remote_copy(
+    while len(heard) < len(reaches):
+        know()
+
+    def spread(i, carry):
+        k = me + i
+        pltpu.make_async_remote_copy(
             src_ref=row, dst_ref=rows.at[i - 1], send_sem=row_send, recv_sem=row_recv,
-            device_id=other(i), device_id_type=MESH)
-
-    def spread(i, carry):
-        to(i).start()
+            device_id=jnp.where(k < n, k, k - n),
+            device_id_type=pl.DeviceIdType.LOGICAL).start()
         return carry
 
     lax.fori_loop(1, n, spread, 0)
@@ -429,8 +465,9 @@
             field, field, field, field,
             pltpu.VMEM((1, width), f32),
             pltpu.VMEM((nx * ny, 1, width), f32),
-            pltpu.VMEM((scen * layers, 2 * width, width), jnp.bfloat16),
-            pltpu.VMEM((5, ext, 2 * width), jnp.bfloat16),
+            pltpu.VMEM((2 * width, width), jnp.bfloat16),
+            pltpu.VMEM((2 * width, width), jnp.bfloat16),
+            pltpu.SemaphoreType.REGULAR((max(nx, ny).bit_length(),)),
             pltpu.SemaphoreType.DMA((4,)),
             pltpu.SemaphoreType.DMA((18,)),
             pltpu.SemaphoreType.DMA((18,)),

time: 22.2 us -> 19.8 us (0.89)
  Pallas kernels: 21.1 us -> 18.8 us
    pallas_call x1, Pallas kernels: 21.1 us -> 18.8 us  [per_device(): pl.pallas_call(functools.partial(kernel, nx, ny), out_shape=pltpu.VMEM(pr...]
where the time goes in v2:
time: 19.8 us; the launch traced here: 19.7 us
  Pallas kernels  18.8 us (95%)
  local copies, waits for them, and re-layouts  0.93 us (5%)
    pallas_call x1, Pallas kernels, per_device(): pl.pallas_call(functools.partial(kernel, nx, ny), out_shape=pltpu.VMEM(pr...  18.8 us
    unnamed x1, local copies, waits for them, and re-layouts  0.93 us

profile of v2, /device:TPU:0, one launch (start us, length us, event | category | flops | bytes accessed | tf_op | source)
XLA Modules:
  0.0 19.7 jit_solution(12198400089127853072)
XLA Ops:
  0.0 18.8 %shard_map.46 = f32[2,7,128,128]{3,2,1,0:T(8,128)S(1)} custom-call(f32[2,7,128,128]{3,2,1,0:T(8,128)} %prev.1, f32[2,4,128,128]{3,2,1,0:T(8,128)} %diss.1, s32[4,128,128]{2,1,0:T(8,128)} %mat.1, s32[3,128,128]{2,1,0:T(8,128)} %cool.1), custom_call_target="tpu_custom_call" | custom-call | tf_op jit(solution)/shard_map/pallas_call | solution.py:450
  18.8 0.9 %copy.6 = f32[2,7,128,128]{3,2,1,0:T(8,128)} copy(f32[2,7,128,128]{3,2,1,0:T(8,128)S(1)} %shard_map.46) | data formatting | bytes 1835008
